TPU v7x, 32 devices: a whole 2x2x4 slice. The times are simulated.
32 devices in a mesh: copy: 2 (over core), fsdp: 4 (over z), tp: 4 (over y, x).
Axes of the slice: x: 2, y: 2, z: 4, core: 2. Of those that a mesh axis runs over, the one named last changes fastest.
Arguments:
- gradients: float32 [32, 128, 4096], P('copy', 'fsdp', 'tp'), parts along dimension 0, may hold values from -6 to 6
- momentum: float32 [32, 128, 4096], P('copy', 'fsdp', 'tp'), parts along dimension 0, may hold values from -6 to 6
- weights: float32 [32, 128, 4096], P('copy', 'fsdp', 'tp'), parts along dimension 0, may hold values from -0.1875 to 0.1875
Outputs:
- new_weights: float32 [32, 128, 4096], P('copy', 'fsdp', 'tp'), parts along dimension 0
- new_momentum: float32 [32, 128, 4096], P('copy', 'fsdp', 'tp'), parts along dimension 0
There are 2 independent parts, one for each index of `copy`. A program takes and returns all parts, laid end to end along the dimension named above; each array names one. Nothing has to cross between parts.
All inputs are finite; a program needn't handle non-finite values.
Results may differ from a plain program's by a relative error of at most 0.00014.
Values sent between devices are 32-bit elements; how exact they have to be, the bound alone decides.
A program may use at most 64 MiB of HBM per device.

v0:
```python
import jax
import jax.numpy as jnp
from jax import lax
from jax.sharding import PartitionSpec as P

ITERS = 4
hold_rate = 0.95
learn_rate = 0.9
decay_rate = 0.1


def mul(a, b):
    return jnp.einsum("mij,mjk->mik", a, b, precision=lax.Precision.HIGHEST)


def mixing(gram):
    eye = jnp.eye(gram.shape[-1], dtype=gram.dtype)
    scale = lax.rsqrt(jnp.sum(gram * eye, axis=(1, 2), keepdims=True) + 1e-06)
    gram = gram * scale * scale
    total = scale * eye
    for step in range(ITERS):
        poly = 3.4445 * eye - 4.775 * gram + 2.0315 * mul(gram, gram)
        total = mul(poly, total)
        if step < ITERS - 1:
            gram = mul(poly, mul(gram, poly))
    return total


def shards(gradients, momentum, weights):
    new_momentum = hold_rate * momentum + gradients
    direction = hold_rate * new_momentum + gradients
    moved = lax.all_to_all(direction, "fsdp", split_axis=0, concat_axis=1, tiled=True)
    gram = jnp.einsum("mik,mjk->mij", moved, moved, precision=lax.Precision.HIGHEST)
    gram = lax.psum(gram, "tp")
    iterate = mul(mixing(gram), moved)
    back = lax.all_to_all(iterate, "fsdp", split_axis=1, concat_axis=0, tiled=True)
    new_weights = (1.0 - learn_rate * decay_rate) * weights - learn_rate * back
    return (new_weights, new_momentum)


def solution(mesh):
    return jax.shard_map(
        shards,
        mesh=mesh,
        in_specs=(P("copy", "fsdp", "tp"), P("copy", "fsdp", "tp"), P("copy", "fsdp", "tp")),
        out_specs=(P("copy", "fsdp", "tp"), P("copy", "fsdp", "tp")),
        check_vma=False,
    )
```

profile of v0, /device:TPU:0, one launch (start us, length us, event | category | flops | bytes accessed | tf_op | source)
XLA Modules:
  0.0 186.5 jit_solution(14155956798188366832)
XLA Ops:
  7.2 0.0 all-reduce.2.cloned.1.call-start
  7.2 4.5 %multiply_add_fusion = (f32[16,32,1024]{2,1,0:T(8,128)S(1)}, f32[16,32,1024]{2,1,0:T(8,128)}) fusion(f32[16,32,1024]{2,1,0:T(8,128)} %param.3, f32[16,32,1024]{2,1,0:T(8,128)} %param.4), kind=kLoop, calls=%fused_computation.1 | loop fusion | flops 2097152 | bytes 8388608 | tf_op jit(solution)/shard_map/add | solution.py:31
  11.7 54.3 %all_to_all.27 = f32[16,32,1024]{2,1,0:T(8,128)S(1)} all-to-all(f32[16,32,1024]{2,1,0:T(8,128)S(1)} %get-tuple-element.2), channel_id=1, replica_groups=mesh['copy'=2,'fsdp'=4,'tp'=4] {'fsdp'}, dimensions={0} | all-to-all | bytes 4194304 | tf_op jit(solution)/shard_map/all_to_all | solution.py:32
  66.0 0.1 copy.7
  66.2 2.8 %fusion.13 = f32[4,128,128]{2,1,0:T(8,128)} fusion(f32[4,128,1024]{2,1,0:T(8,128)S(1)} %bitcast.37), kind=kOutput, calls=%fused_computation.25 | convolution fusion | flops 805306368 | bytes 2359296 | tf_op jit(solution)/shard_map/mik,mjk->mij/dot_general | solution.py:33
  68.9 0.0 all-reduce.2.cloned.1.call-update
  69.0 42.4 %all-reduce.2.cloned.1.call-done = f32[4,128,128]{2,1,0:T(8,128)} async-done(((f32[4,128,128]{2,1,0:T(8,128)}), f32[4,128,128]{2,1,0:T(8,128)}) %all-reduce.2.cloned.1.call-update) | async-done | bytes 262160 | tf_op jit(solution)/shard_map/psum | solution.py:34
  111.4 1.1 multiply_reduce_fusion
  112.5 1.6 fusion.3
  114.1 0.4 fusion.4
  114.6 1.4 fusion.6
  116.0 0.4 fusion.14
  116.4 0.4 fusion.2
  116.7 0.4 fusion.15
  117.1 0.4 fusion.19
  117.5 0.4 fusion.16
  118.0 0.4 fusion.1
  118.3 0.4 fusion.17
  118.7 0.4 fusion.20
  119.1 0.4 fusion.18
  119.5 0.4 fusion
  119.9 0.4 fusion.21
  120.3 1.9 %fusion.22 = f32[4,128,1024]{2,1,0:T(8,128)S(1)} fusion(f32[4,128,128]{2,1,0:T(8,128)S(1)} %fusion.21, f32[4,128,1024]{2,1,0:T(8,128)S(1)} %bitcast.38), kind=kOutput, calls=%fused_computation.34 | convolution fusion | flops 805306368 | bytes 4456448 | tf_op jit(solution)/shard_map/mij,mjk->mik/dot_general | solution.py:13
  122.3 1.4 copy.8
  123.6 52.1 %all_to_all.28 = f32[4,128,1024]{2,0,1:T(4,128)S(1)} all-to-all(f32[4,128,1024]{2,0,1:T(4,128)S(1)} %copy.8), channel_id=1, replica_groups=mesh['copy'=2,'fsdp'=4,'tp'=4] {'fsdp'}, dimensions={1} | all-to-all | bytes 4194304 | tf_op jit(solution)/shard_map/all_to_all | solution.py:36
  175.7 0.6 broadcast_multiply_fusion
  176.3 0.0 copy-start
  176.3 1.2 copy.9
  177.6 0.4 copy-done
  177.9 1.8 bitcast_subtract_fusion
  (3 shorter events, 0.0 us)
Async XLA Ops:
  7.2 104.2 %all-reduce.2.cloned.1.call-start = ((), (), s32[]{:S(2)}) async-start(), calls=%async_computation.2 | async-start | bytes 524288 | tf_op jit(solution)/shard_map/psum | solution.py:34
  176.3 1.6 copy-start
Sparse Core Ops, SparseCore 0:
  69.1 42.2 all-reduce.1
where the time goes:
time: 187 us
  blocking collectives  106 us (57%)
  waiting for transfers between devices  42.4 us (23%)
  between operations  14.2 us (8%)
  matrix products  12.4 us (7%)
  other arithmetic  7.95 us (4%)
  local copies, waits for them, and re-layouts  3.07 us (2%)
    all_to_all x1, blocking collectives, shards(): lax.all_to_all(direction, 'fsdp', split_axis=0, concat_axis=1, tiled=True)  54.3 us
    all_to_all x1, blocking collectives, shards(): lax.all_to_all(iterate, 'fsdp', split_axis=1, concat_axis=0, tiled=True)  52.1 us
    psum x1, waiting for transfers between devices, shards(): gram = lax.psum(gram, 'tp')  42.4 us
    dot_general x15, matrix products, mul(): return jnp.einsum('mij,mjk->mik', a, b, precision=lax.Precision.HIGHEST)  9.65 us
    add x1, other arithmetic, shards(): direction = hold_rate * new_momentum + gradients  4.5 us
  transfers between devices with their start and end apart: 1, of which 1 were waited for; matrix products, arithmetic and copies ran while one was open for 0% of the time, Pallas kernels for 0%

commit v1 on v0

--- a/solution.py
+++ b/solution.py
@@ -31,7 +31,11 @@
     direction = hold_rate * new_momentum + gradients
     moved = lax.all_to_all(direction, "fsdp", split_axis=0, concat_axis=1, tiled=True)
     gram = jnp.einsum("mik,mjk->mij", moved, moved, precision=lax.Precision.HIGHEST)
-    gram = lax.psum(gram, "tp")
+    num = lax.psum(1, "tp")
+    aux = gram
+    for dd in [[(jj, jj ^ q) for jj in range(num)] for q in (1, 2, 4, 8, 16) if q < num]:
+        aux = aux + lax.ppermute(aux, "tp", dd)
+    gram = aux
     iterate = mul(mixing(gram), moved)
     back = lax.all_to_all(iterate, "fsdp", split_axis=1, concat_axis=0, tiled=True)
     new_weights = (1.0 - learn_rate * decay_rate) * weights - learn_rate * back

time: 187 us -> 138 us (0.74)
  waiting for transfers between devices: 42.4 us -> 10.3 us
  between operations: 14.2 us -> 0.81 us
  starting transfers between devices: 0.04 us -> 3.14 us
  matrix products: 12.4 us -> 9.63 us
  blocking collectives: 106 us -> 104 us
    psum x1 -> x0, waiting for transfers between devices: 42.4 us -> none  [shards(): gram = lax.psum(gram, 'tp')]
    ppermute x0 -> x2, waiting for transfers between devices: none -> 10.3 us  [shards(): aux = aux + lax.ppermute(aux, 'tp', dd)]
    ppermute x0 -> x2, starting transfers between devices: none -> 3.14 us  [shards(): aux = aux + lax.ppermute(aux, 'tp', dd)]
    all_to_all x1, blocking collectives: 52.1 us -> 49.8 us  [shards(): lax.all_to_all(iterate, 'fsdp', split_axis=1, concat_axis=0, tiled=True)]
    dot_general x15, matrix products: 9.65 us -> 7.58 us  [mul(): return jnp.einsum('mij,mjk->mik', a, b, precision=lax.Precision.HIGHEST)]
  transfers between devices with their start and end apart: 1 -> 2, of which waited for: 1 -> 2; matrix products, arithmetic and copies ran while one was open for 0% -> 0% of each run, Pallas kernels for 0% -> 0%
where the time goes in v1:
time: 138 us
  blocking collectives  104 us (75%)
  waiting for transfers between devices  10.3 us (7%)
  matrix products  9.63 us (7%)
  other arithmetic  6.91 us (5%)
  local copies, waits for them, and re-layouts  3.17 us (2%)
  starting transfers between devices  3.14 us (2%)
    all_to_all x1, blocking collectives, shards(): lax.all_to_all(direction, 'fsdp', split_axis=0, concat_axis=1, tiled=True)  54.3 us
    all_to_all x1, blocking collectives, shards(): lax.all_to_all(iterate, 'fsdp', split_axis=1, concat_axis=0, tiled=True)  49.8 us
    ppermute x2, waiting for transfers between devices, shards(): aux = aux + lax.ppermute(aux, 'tp', dd)  10.3 us
    dot_general x15, matrix products, mul(): return jnp.einsum('mij,mjk->mik', a, b, precision=lax.Precision.HIGHEST)  7.58 us
    add x1, other arithmetic, shards(): direction = hold_rate * new_momentum + gradients  4.27 us
    ppermute x2, starting transfers between devices, shards(): aux = aux + lax.ppermute(aux, 'tp', dd)  3.14 us
  transfers between devices with their start and end apart: 2, of which 2 were waited for; matrix products, arithmetic and copies ran while one was open for 0% of the time, Pallas kernels for 0%

profile of v1, /device:TPU:0, one launch (start us, length us, event | category | flops | bytes accessed | tf_op | source)
XLA Modules:
  0.0 138.0 jit_solution(11490770226001014746)
XLA Ops:
  0.6 4.3 %multiply_add_fusion = (f32[16,32,1024]{2,1,0:T(8,128)S(1)}, f32[16,32,1024]{2,1,0:T(8,128)}) fusion(f32[16,32,1024]{2,1,0:T(8,128)} %param.3, f32[16,32,1024]{2,1,0:T(8,128)} %param.4), kind=kLoop, calls=%fused_computation.1 | loop fusion | flops 2097152 | bytes 8388608 | tf_op jit(solution)/shard_map/add | solution.py:31
  4.9 54.3 %all_to_all.27 = f32[16,32,1024]{2,1,0:T(8,128)S(1)} all-to-all(f32[16,32,1024]{2,1,0:T(8,128)S(1)} %get-tuple-element.4), channel_id=1, replica_groups=mesh['copy'=2,'fsdp'=4,'tp'=4] {'fsdp'}, dimensions={0} | all-to-all | bytes 4194304 | tf_op jit(solution)/shard_map/all_to_all | solution.py:32
  59.2 0.2 copy.7
  59.5 2.1 %fusion.12 = f32[4,128,128]{2,1,0:T(8,128)S(1)} fusion(f32[4,128,1024]{2,1,0:T(8,128)S(1)} %bitcast.37), kind=kOutput, calls=%fused_computation.25 | convolution fusion | flops 805306368 | bytes 2359296 | tf_op jit(solution)/shard_map/mik,mjk->mij/dot_general | solution.py:33
  61.5 1.6 %collective-permute-start = (f32[4,128,128]{2,1,0:T(8,128)S(1)}, f32[4,128,128]{2,1,0:T(8,128)S(1)}, u32[]{:S(2)}, u32[]{:S(2)}) collective-permute-start(f32[4,128,128]{2,1,0:T(8,128)S(1)} %fusion.12), channel_id=1, source_target_pairs={{0,1},{1,0},{2,3},{3,2},{4,5},{5,4},{6,7},{7,6},{8,9},{9,8},{10,11... | collective-permute-start | bytes 786440 | tf_op jit(solution)/shard_map/ppermute | solution.py:37
  63.1 5.5 %collective-permute-done = f32[4,128,128]{2,1,0:T(8,128)S(1)} collective-permute-done((f32[4,128,128]{2,1,0:T(8,128)S(1)}, f32[4,128,128]{2,1,0:T(8,128)S(1)}, u32[]{:S(2)}, u32[]{:S(2)}) %collective-permute-start) | collective-permute-done | bytes 262176 | tf_op jit(solution)/shard_map/ppermute | solution.py:37
  68.6 1.6 %collective-permute-start.1 = (f32[4,128,128]{2,1,0:T(8,128)S(1)}, f32[4,128,128]{2,1,0:T(8,128)S(1)}, u32[]{:S(2)}, u32[]{:S(2)}) collective-permute-start(f32[4,128,128]{2,1,0:T(8,128)S(1)} %add.34), channel_id=1, source_target_pairs={{0,2},{1,3},{2,0},{3,1},{4,6},{5,7},{6,4},{7,5},{8,10},{9,11},{10,... | collective-permute-start | bytes 786440 | tf_op jit(solution)/shard_map/ppermute | solution.py:37
  70.2 4.8 %collective-permute-done.1 = f32[4,128,128]{2,1,0:T(8,128)S(1)} collective-permute-done((f32[4,128,128]{2,1,0:T(8,128)S(1)}, f32[4,128,128]{2,1,0:T(8,128)S(1)}, u32[]{:S(2)}, u32[]{:S(2)}) %collective-permute-start.1) | collective-permute-done | bytes 262176 | tf_op jit(solution)/shard_map/ppermute | solution.py:37
  75.1 0.1 multiply_reduce_fusion
  75.2 0.5 subtract_add_fusion
  75.7 0.4 fusion.5
  76.1 0.4 fusion.3
  76.6 0.4 fusion.13
  77.0 0.4 fusion.2
  77.4 0.4 fusion.14
  77.8 0.4 fusion.18
  78.2 0.4 fusion.15
  78.6 0.4 fusion.1
  79.0 0.4 fusion.16
  79.4 0.4 fusion.19
  79.8 0.4 fusion.17
  80.2 0.4 fusion
  80.6 0.4 fusion.20
  81.0 1.9 %fusion.21 = f32[4,128,1024]{2,1,0:T(8,128)S(1)} fusion(f32[4,128,128]{2,1,0:T(8,128)S(1)} %fusion.20, f32[4,128,1024]{2,1,0:T(8,128)S(1)} %bitcast.38), kind=kOutput, calls=%fused_computation.34 | convolution fusion | flops 805306368 | bytes 4456448 | tf_op jit(solution)/shard_map/mij,mjk->mik/dot_general | solution.py:13
  82.9 1.4 copy.8
  84.3 49.8 %all_to_all.28 = f32[4,128,1024]{2,0,1:T(4,128)S(1)} all-to-all(f32[4,128,1024]{2,0,1:T(4,128)S(1)} %copy.8), channel_id=1, replica_groups=mesh['copy'=2,'fsdp'=4,'tp'=4] {'fsdp'}, dimensions={1} | all-to-all | bytes 4194304 | tf_op jit(solution)/shard_map/all_to_all | solution.py:40
  134.0 0.7 broadcast_multiply_fusion
  134.7 0.0 copy-start
  134.7 1.2 copy.9
  135.9 0.4 copy-done
  136.3 1.8 %bitcast_subtract_fusion = f32[16,32,1024]{2,1,0:T(8,128)} fusion(f32[4,4,32,1024]{3,2,1,0:T(8,128)S(1)} %copy.9, f32[16,32,1024]{2,1,0:T(8,128)S(1)} %copy-done), kind=kLoop, calls=%fused_computation | loop fusion | flops 1048576 | bytes 6291456 | tf_op jit(solution)/shard_map/sub | solution.py:41
  (4 shorter events, 0.1 us)
Async XLA Ops:
  61.5 7.0 %collective-permute-start = (f32[4,128,128]{2,1,0:T(8,128)S(1)}, f32[4,128,128]{2,1,0:T(8,128)S(1)}, u32[]{:S(2)}, u32[]{:S(2)}) collective-permute-start(f32[4,128,128]{2,1,0:T(8,128)S(1)} %fusion.12), channel_id=1, source_target_pairs={{0,1},{1,0},{2,3},{3,2},{4,5},{5,4},{6,7},{7,6},{8,9},{9,8},{10,11... | collective-permute-start | bytes 786440 | tf_op jit(solution)/shard_map/ppermute | solution.py:37
  68.6 6.4 %collective-permute-start.1 = (f32[4,128,128]{2,1,0:T(8,128)S(1)}, f32[4,128,128]{2,1,0:T(8,128)S(1)}, u32[]{:S(2)}, u32[]{:S(2)}) collective-permute-start(f32[4,128,128]{2,1,0:T(8,128)S(1)} %add.34), channel_id=1, source_target_pairs={{0,2},{1,3},{2,0},{3,1},{4,6},{5,7},{6,4},{7,5},{8,10},{9,11},{10,... | collective-permute-start | bytes 786440 | tf_op jit(solution)/shard_map/ppermute | solution.py:37
  134.7 1.6 %copy-start = (f32[16,32,1024]{2,1,0:T(8,128)S(1)}, f32[16,32,1024]{2,1,0:T(8,128)}, u32[]{:S(2)}) copy-start(f32[16,32,1024]{2,1,0:T(8,128)} %param.5) | copy-start | bytes 6291460
